TPU v7x, 32 devices: a whole 2x2x4 slice. The times are simulated.
32 devices in a mesh: dp: 4 (over z), expert: 8 (over y, x, core).
Axes of the slice: x: 2, y: 2, z: 4, core: 2. Of those that a mesh axis runs over, the one named last changes fastest.
Arguments:
- tokens: bfloat16 [32768, 2080], P(('dp', 'expert')), may hold values from -6 to 6
- router_logits: bfloat16 [32768, 2048], P(('dp', 'expert')), may hold values from -300 to 300
- gate_grad: float32 [32768], P(('dp', 'expert')), may hold values from -6 to 6
- expert_index: int32 [32768, 1], P(('dp', 'expert')), may hold values from 0 to 2047
- keep_mask: int32 [2048], replicated, may hold values 0 or 1
Outputs:
- router_grad: float32 [2048, 2080], P('expert', 'dp')
All inputs are finite; a program needn't handle non-finite values.
Results may differ from a plain program's by a relative error of at most 0.0003.
Values sent between devices are 32-bit elements; how exact they have to be, the bound alone decides.
No kernel may reach another device: no remote copies, remote signals or barrier semaphores. Data moves between devices by JAX's collectives and lax.ppermute only.
A program may use at most 128 MiB of HBM per device.

v0:
```python
import math

import jax
import jax.numpy as jnp
from jax import lax
from jax.sharding import PartitionSpec as P


def make_term(grad_source, wide_tokens):
    return lax.dot_general(
        grad_source,
        wide_tokens,
        (((0,), (0,)), ((), ())),
        precision=lax.Precision.HIGHEST,
        preferred_element_type=jnp.float32,
    )


def local(tokens, router_logits, gate_grad, expert_index, keep_mask):
    tok_rows = tokens.shape[0]
    expert_total = router_logits.shape[1]
    dp_width = lax.axis_size("dp")
    expert_width = lax.axis_size("expert")
    total_tokens = tok_rows * dp_width * expert_width
    block_rows = math.gcd(tok_rows, 512)
    block_count = tok_rows // block_rows
    routed = expert_index[:, 0].reshape(block_count, block_rows)
    logit_blocks = router_logits.reshape(block_count, block_rows, expert_total)
    gate_blocks = gate_grad.reshape(block_count, block_rows)

    def block_counts(routed_block):
        columns = lax.broadcasted_iota(jnp.int32, (block_rows, expert_total), 1)
        return jnp.sum((columns == routed_block[:, None]).astype(jnp.int32), axis=0)

    local_counts = jnp.sum(lax.map(block_counts, routed), axis=0)
    counts = lax.psum(local_counts, ("dp", "expert"))
    aux_cost = counts.astype(jnp.float32) * (expert_total / total_tokens)
    kept_cols = keep_mask.astype(jnp.float32)

    def block_grad(inputs):
        logit_block, gate_block, routed_block = inputs
        scores = logit_block.astype(jnp.float32)
        row_peak = jnp.max(scores, axis=1, keepdims=True)
        weights = jnp.exp(scores - row_peak)
        router_probs = weights / jnp.sum(weights, axis=1, keepdims=True)
        columns = lax.broadcasted_iota(jnp.int32, scores.shape, 1)
        chosen = columns == routed_block[:, None]
        top_prob = jnp.sum(jnp.where(chosen, router_probs, 0.0), axis=1)
        spread = jnp.dot(router_probs, aux_cost, precision=lax.Precision.HIGHEST)
        gate_part = (gate_block * top_prob)[:, None] * (chosen.astype(jnp.float32) - router_probs)
        aux_part = router_probs * (aux_cost[None, :] - spread[:, None])
        return kept_cols[None, :] * (gate_part + aux_part)

    logit_grad = lax.map(block_grad, (logit_blocks, gate_blocks, routed)).reshape(
        tok_rows, expert_total
    )
    wide_tokens = tokens.astype(jnp.float32)
    owned = lax.psum_scatter(
        make_term(logit_grad, wide_tokens), "expert", scatter_dimension=0, tiled=True
    )
    result = lax.psum_scatter(owned, "dp", scatter_dimension=1, tiled=True)
    return result


def solution(mesh):
    in_specs = (
        P(("dp", "expert"), None),
        P(("dp", "expert"), None),
        P(("dp", "expert")),
        P(("dp", "expert"), None),
        P(),
    )
    out_specs = P("expert", "dp")
    return jax.shard_map(local, mesh=mesh, in_specs=in_specs, out_specs=out_specs, check_vma=False)
```

profile of v0, /device:TPU:0, one launch (start us, length us, event | category | flops | bytes accessed | tf_op | source)
XLA Modules:
  0.0 290.1 jit_solution(12523892745936666752)
XLA Ops:
  6.5 0.0 reduce-scatter.3.cloned.1.call-start
  6.5 0.5 broadcast.96
  7.0 1.3 reduce.8
  8.3 0.7 reshape.138
  9.0 0.7 convert_element_type.38
  9.7 1.4 while.22
  9.7 0.6 convert_reduce_fusion.2
  10.3 0.1 dynamic_update_slice.14
  10.4 0.6 convert_reduce_fusion.2
  11.0 0.1 dynamic_update_slice.14
  11.1 42.1 %psum.7 = s32[2048]{0:T(1024)S(1)} all-reduce(s32[2048]{0:T(1024)S(1)} %reduce_sum.42), channel_id=1, replica_groups=mesh['dp'=4,'expert'=8] {'dp','expert'}, use_global_device_ids=true, to_apply=%region_4.5 | all-reduce | flops 2048 | bytes 16384 | tf_op jit(solution)/shard_map/psum | solution.py:36
  53.2 33.4 %while.23 = (s32[]{:T(128)}, f32[2,512,2048]{2,1,0:T(8,128)}, f32[2048]{0:T(1024)S(1)}, f32[2,512]{1,0:T(2,128)S(1)}, s32[2,512]{1,0:T(2,128)S(1)}, /*index=5*/b...) while((s32[]{:T(128)}, f32[2,512,2048]{2,1,0:T(8,128)}, f32[2048]{0:T(1024)S(1)}, ...), condition=%wide.region_9.10_spmd, body=%wide.region_5.9_spmd.sunk | while | flops 37748224 | bytes 90249440 | solution.py:54
  53.2 0.0 copy-start
  53.2 2.1 dynamic-slice_reduce_fusion.2
  55.3 0.0 slice-start
  55.3 2.6 fusion.22
  57.9 0.0 copy-done
  57.9 0.0 slice-start.1
  57.9 4.4 %fusion.23 = f32[1,512]{1,0:T(1,128)S(1)} fusion(f32[2048,1]{0,1:T(1,128)S(1)} %bitcast.48, f32[512]{0:T(512)S(1)} %fusion.22, f32[512]{0:T(512)S(1)} %reduce_max.18, bf16[2,512,2048]{2,1,0:T(8,128)(2,1)S(1)} %copy-done, s32[]{:T(128)S(6)} %copy.16), kind=kOutput, calls=%fused_computation.15.clone.1 | convolution fusion | flops 15728640 | bytes 2111492 | tf_op jit(solution)/shard_map/while/body/eval_jaxpr/dot_general | solution.py:49
  62.3 1.7 select_reduce_fusion.2
  64.0 0.0 slice-done
  64.0 0.0 slice-done.1
  64.0 2.6 multiply_dynamic-update-slice_fusion.2
  66.7 0.0 copy-start.1
  66.7 3.2 %copy-done.1 = f32[2,512,2048]{2,1,0:T(8,128)} copy-done((f32[2,512,2048]{2,1,0:T(8,128)}, f32[2,512,2048]{2,1,0:T(8,128)S(1)}, u32[]{:S(2)}) %copy-start.1) | copy-done | bytes 8388632 | tf_op jit(solution)/shard_map/while
  69.9 0.0 copy-start
  69.9 2.1 dynamic-slice_reduce_fusion.2
  72.0 0.0 slice-start
  72.0 2.6 fusion.22
  74.6 0.0 copy-done
  74.6 0.0 slice-start.1
  74.6 4.4 %fusion.23 = f32[1,512]{1,0:T(1,128)S(1)} fusion(f32[2048,1]{0,1:T(1,128)S(1)} %bitcast.48, f32[512]{0:T(512)S(1)} %fusion.22, f32[512]{0:T(512)S(1)} %reduce_max.18, bf16[2,512,2048]{2,1,0:T(8,128)(2,1)S(1)} %copy-done, s32[]{:T(128)S(6)} %copy.16), kind=kOutput, calls=%fused_computation.15.clone.1 | convolution fusion | flops 15728640 | bytes 2111492 | tf_op jit(solution)/shard_map/while/body/eval_jaxpr/dot_general | solution.py:49
  79.0 1.7 select_reduce_fusion.2
  80.7 0.0 slice-done
  80.7 0.0 slice-done.1
  80.7 2.6 multiply_dynamic-update-slice_fusion.2
  83.4 0.0 copy-start.1
  83.4 3.2 %copy-done.1 = f32[2,512,2048]{2,1,0:T(8,128)} copy-done((f32[2,512,2048]{2,1,0:T(8,128)}, f32[2,512,2048]{2,1,0:T(8,128)S(1)}, u32[]{:S(2)}) %copy-start.1) | copy-done | bytes 8388632 | tf_op jit(solution)/shard_map/while
  86.6 32.6 %fusion.12 = f32[2048,2080]{0,1:T(8,128)} fusion(f32[1024,2048]{1,0:T(8,128)} %bitcast.55, bf16[1024,2080]{0,1:T(8,128)(2,1)} %param.9), kind=kOutput, calls=%fused_computation.24 | convolution fusion | flops 52344913920 | bytes 29687808 | tf_op jit(solution)/shard_map/dot_general | solution.py:10
  119.2 0.0 reduce-scatter.3.cloned.1.call-update
  119.2 0.0 reduce-scatter.5.cloned.1.call-start
  119.3 117.4 %reduce-scatter.3.cloned.1.call-done = f32[256,2080]{0,1:T(8,128)} async-done(((f32[2048,2080]{0,1:T(8,128)}), f32[256,2080]{0,1:T(8,128)}) %reduce-scatter.3.cloned.1.call-update) | async-done | bytes 2129936 | tf_op jit(solution)/shard_map/reduce_scatter | solution.py:58
  236.7 0.0 reduce-scatter.5.cloned.1.call-update
  236.8 46.5 %reduce-scatter.5.cloned.1.call-done = f32[256,520]{0,1:T(8,128)} async-done(((f32[256,2080]{0,1:T(8,128)}), f32[256,520]{0,1:T(8,128)}) %reduce-scatter.5.cloned.1.call-update) | async-done | bytes 532496 | tf_op jit(solution)/shard_map/reduce_scatter | solution.py:61
  (17 shorter events, 0.1 us)
Async XLA Ops:
  6.5 230.2 %reduce-scatter.3.cloned.1.call-start = ((), (), s32[]{:S(2)}) async-start(), calls=%async_computation.2 | async-start | bytes 19169280 | tf_op jit(solution)/shard_map/reduce_scatter | solution.py:58
  53.2 4.7 %copy-start = (bf16[2,512,2048]{2,1,0:T(8,128)(2,1)S(1)}, bf16[2,512,2048]{2,1,0:T(8,128)(2,1)}, u32[]{:S(2)}) copy-start(bf16[2,512,2048]{2,1,0:T(8,128)(2,1)} %get-tuple-element.231) | copy-start | bytes 12582916 | tf_op jit(solution)/shard_map/while
  55.3 8.7 %slice-start = ((s8[8388608]{0:T(1024)(128)(4,1)}), s8[4194304]{0:T(1024)(128)(4,1)S(1)}, s32[]{:S(2)}) async-start(s8[8388608]{0:T(1024)(128)(4,1)} %bitcast.53), calls=%async_computation.4 | async-start | bytes 8388608 | tf_op jit(solution)/shard_map/while
  57.9 6.1 %slice-start.1 = ((s8[8388608]{0:T(1024)(128)(4,1)}), s8[4194304]{0:T(1024)(128)(4,1)S(1)}, s32[]{:S(2)}) async-start(s8[8388608]{0:T(1024)(128)(4,1)} %bitcast.53), calls=%async_computation.5 | async-start | bytes 8388608 | tf_op jit(solution)/shard_map/while
  66.7 3.2 %copy-start.1 = (f32[2,512,2048]{2,1,0:T(8,128)}, f32[2,512,2048]{2,1,0:T(8,128)S(1)}, u32[]{:S(2)}) copy-start(f32[2,512,2048]{2,1,0:T(8,128)S(1)} %multiply_dynamic-update-slice_fusion.2) | copy-start | bytes 25165828 | tf_op jit(solution)/shard_map/while
  69.9 4.7 %copy-start = (bf16[2,512,2048]{2,1,0:T(8,128)(2,1)S(1)}, bf16[2,512,2048]{2,1,0:T(8,128)(2,1)}, u32[]{:S(2)}) copy-start(bf16[2,512,2048]{2,1,0:T(8,128)(2,1)} %get-tuple-element.231) | copy-start | bytes 12582916 | tf_op jit(solution)/shard_map/while
  72.0 8.7 %slice-start = ((s8[8388608]{0:T(1024)(128)(4,1)}), s8[4194304]{0:T(1024)(128)(4,1)S(1)}, s32[]{:S(2)}) async-start(s8[8388608]{0:T(1024)(128)(4,1)} %bitcast.53), calls=%async_computation.4 | async-start | bytes 8388608 | tf_op jit(solution)/shard_map/while
  74.6 6.1 %slice-start.1 = ((s8[8388608]{0:T(1024)(128)(4,1)}), s8[4194304]{0:T(1024)(128)(4,1)S(1)}, s32[]{:S(2)}) async-start(s8[8388608]{0:T(1024)(128)(4,1)} %bitcast.53), calls=%async_computation.5 | async-start | bytes 8388608 | tf_op jit(solution)/shard_map/while
  83.4 3.2 %copy-start.1 = (f32[2,512,2048]{2,1,0:T(8,128)}, f32[2,512,2048]{2,1,0:T(8,128)S(1)}, u32[]{:S(2)}) copy-start(f32[2,512,2048]{2,1,0:T(8,128)S(1)} %multiply_dynamic-update-slice_fusion.2) | copy-start | bytes 25165828 | tf_op jit(solution)/shard_map/while
  119.2 164.0 %reduce-scatter.5.cloned.1.call-start = ((), (), s32[]{:S(2)}) async-start(), calls=%async_computation.3 | async-start | bytes 2662400 | tf_op jit(solution)/shard_map/reduce_scatter | solution.py:61
Sparse Core Ops, SparseCore 0:
  119.4 117.3 reduce-scatter.2
  239.0 44.1 reduce-scatter.4
where the time goes:
time: 291 us; the launch traced here: 290 us
  waiting for transfers between devices  164 us (56%)
  blocking collectives  42.1 us (14%)
  matrix products  41.4 us (14%)
  other arithmetic  21.1 us (7%)
  between operations  13.4 us (5%)
  local copies, waits for them, and re-layouts  7.88 us (3%)
    reduce_scatter x1, waiting for transfers between devices, local(): lax.psum_scatter(make_term(logit_grad, wide_tokens), 'expert', scatter_di...  117 us
    reduce_scatter x1, waiting for transfers between devices, local(): result = lax.psum_scatter(owned, 'dp', scatter_dimension=1, tiled=True)  46.5 us
    psum x1, blocking collectives, local(): counts = lax.psum(local_counts, ('dp', 'expert'))  42.1 us
    dot_general x1, matrix products, make_term(): lax.dot_general(grad_source, wide_tokens, (((0,), (0,)), ((), ())), preci...  32.6 us
    dot_general x2, matrix products, block_grad(): spread = jnp.dot(router_probs, aux_cost, precision=lax.Precision.HIGHEST)  8.72 us
    while x16, local copies, waits for them, and re-layouts  6.45 us
  transfers between devices with their start and end apart: 2, of which 2 were waited for; matrix products, arithmetic and copies ran while one was open for 0% of the time, Pallas kernels for 0%

commit v1 on v0

v1 whole, which is shorter than its diff:
```python
import functools

import jax
import jax.numpy as jnp
from jax import lax
from jax.experimental import pallas as pl
from jax.experimental.pallas import tpu as pltpu
from jax.sharding import PartitionSpec as P


LANES = 128
SUBLANES = 8


def widths():
    return lax.axis_size("dp"), lax.axis_size("expert")


def local_counts(routed, expert_total):
    high = routed // LANES
    low = routed % LANES
    rows = expert_total // LANES
    high_hot = (high[:, None] == jnp.arange(rows)[None, :]).astype(jnp.bfloat16)
    low_hot = (low[:, None] == jnp.arange(LANES)[None, :]).astype(jnp.bfloat16)
    found = lax.dot_general(
        high_hot, low_hot, (((0,), (0,)), ((), ())), preferred_element_type=jnp.float32
    )
    return found.astype(jnp.int32)


def exchange(value, axis, mask):
    size = lax.axis_size(axis)
    return lax.ppermute(value, axis, [(i, i ^ mask) for i in range(size)])


def global_counts(counts):
    dp_width, expert_width = widths()
    counts = counts + exchange(counts, "expert", 1)
    counts = sum((exchange(counts, "expert", m) for m in range(2, expert_width, 2)), counts)
    return sum((exchange(counts, "dp", m) for m in range(1, dp_width)), counts)


def tiles(width):
    return [slice(k, k + LANES) for k in range(0, width, LANES)]


def down(row):
    return jnp.broadcast_to(row, (LANES, LANES)).T


def across(column):
    return column.T[:1, :]


def total_of(parts):
    return jnp.broadcast_to(jnp.sum(parts, axis=1, keepdims=True), parts.shape)


def lane_places(shape):
    return lax.broadcasted_iota(jnp.int32, shape, 1)


def softmax_kernel(logits_ref, routed_ref, gate_ref, peak_ref, inverse_ref, scale_ref):
    row = pl.ds(pl.program_id(0), 1)
    spans = tiles(logits_ref.shape[1])
    peak = None
    for lanes in spans:
        scores = logits_ref[:, lanes].astype(jnp.float32)
        peak = scores if peak is None else jnp.maximum(peak, scores)
    peak = jnp.broadcast_to(jnp.max(peak, axis=1, keepdims=True), peak.shape)
    routed = down(routed_ref[row, :]) - lane_places(peak.shape)
    total = jnp.zeros_like(peak)
    top = jnp.zeros_like(peak)
    for lanes in spans:
        weights = jnp.exp(logits_ref[:, lanes].astype(jnp.float32) - peak)
        total += weights
        top += jnp.where(routed == lanes.start, weights, 0.0)
    inverse = 1.0 / across(total_of(total))
    peak_ref[row, :] = across(peak)
    inverse_ref[row, :] = inverse
    scale_ref[row, :] = across(total_of(top)) * inverse * gate_ref[row, :]


def softmax(router_logits, routed, gate_grad):
    rows, experts = router_logits.shape
    blocks = rows // LANES
    wide = pl.BlockSpec((LANES, experts), lambda i: (i, 0))
    thin = pl.BlockSpec((blocks, LANES), lambda i: (0, 0))
    return pl.pallas_call(
        softmax_kernel,
        grid=(blocks,),
        in_specs=[wide, thin, thin],
        out_specs=[thin] * 3,
        out_shape=[jax.ShapeDtypeStruct((blocks, LANES), jnp.float32)] * 3,
        cost_estimate=pl.CostEstimate(
            flops=20 * rows * experts, bytes_accessed=2 * rows * experts, transcendentals=rows * experts
        ),
        name="softmax",
    )(router_logits, routed, gate_grad)


def grad_block(unit, index, refs, probs_ref, store):
    logits_ref, routed_ref, peak_ref, inverse_ref, scale_ref, counts_ref, keep_ref = refs
    row = pl.ds(index, 1)
    spans = tiles(logits_ref.shape[1])
    peak = down(peak_ref[row, :])
    inverse = down(inverse_ref[row, :])
    spread = jnp.zeros_like(peak)
    for lanes in spans:
        aux = counts_ref[:, lanes].astype(jnp.float32) * unit
        probs = jnp.exp(logits_ref[:, lanes].astype(jnp.float32) - peak) * inverse
        probs_ref[:, lanes] = probs
        spread += probs * aux
    spread = total_of(spread)
    scale = down(scale_ref[row, :])
    routed = down(routed_ref[row, :]) - lane_places(spread.shape)
    for lanes in spans:
        aux = counts_ref[:, lanes].astype(jnp.float32) * unit
        probs = probs_ref[:, lanes]
        chosen = jnp.where(routed == lanes.start, 1.0, 0.0)
        grad = scale * (chosen - probs) + probs * (aux - spread)
        grad = keep_ref[:, lanes].astype(jnp.float32) * grad
        high = grad.astype(jnp.bfloat16)
        low = (grad - high.astype(jnp.float32)).astype(jnp.bfloat16)
        store(lanes, high, low)


def grad_kernel(unit, *refs):
    high_ref, low_ref, probs_ref = refs[-3:]

    def store(lanes, high, low):
        high_ref[:, lanes] = high
        low_ref[:, lanes] = low

    grad_block(unit, pl.program_id(0), refs[:-3], probs_ref, store)


def logit_grad(logits, routed, stats, counts, keep_mask, unit):
    rows, experts = logits.shape
    blocks = rows // LANES
    wide = pl.BlockSpec((LANES, experts), lambda i: (i, 0))
    thin = pl.BlockSpec((blocks, LANES), lambda i: (0, 0))
    flat = pl.BlockSpec((1, experts), lambda i: (0, 0))
    return pl.pallas_call(
        functools.partial(grad_kernel, unit),
        grid=(blocks,),
        in_specs=[wide, thin, thin, thin, thin, flat, flat],
        out_specs=[wide, wide],
        out_shape=[jax.ShapeDtypeStruct((rows, experts), jnp.bfloat16)] * 2,
        scratch_shapes=[pltpu.VMEM((LANES, experts), jnp.float32)],
        cost_estimate=pl.CostEstimate(
            flops=20 * rows * experts, bytes_accessed=8 * rows * experts, transcendentals=0
        ),
        name="logit_grad",
    )(logits, routed, *stats, counts, keep_mask)


class Walk:
    def __init__(self, half, core, lefts, experts, cols, zblocks, shift):
        self.half, self.core, self.shift = half, core, shift
        self.cols, self.experts, self.zblocks = cols, experts, zblocks
        self.rows = [left.shape[0] // zblocks for left in lefts]
        self.tokens = lefts[0].shape[1]

    def place(self, s):
        s = jnp.maximum(s - self.shift, 0)
        half = self.half
        low = jnp.where(s < 2, half, 1 - half)
        high = jnp.where(jnp.logical_or(s == 0, s == 3), 1 - half, half)
        return low, high

    def block_of(self, s, me):
        low, high = self.place(s)
        return jnp.bitwise_xor(me, self.core + 2 * low + 4 * high)

    def left_specs(self):
        full = [pl.BlockSpec((self.zblocks * r, self.tokens), lambda s, me: (0, 0)) for r in self.rows[:2]]
        part = pl.BlockSpec(
            (self.zblocks // 2 * self.rows[2], self.tokens), lambda s, me, half=self.half: (half, 0)
        )
        return full + [part]

    def out_specs(self):
        half, shift = self.half, self.shift
        deep = self.zblocks // 2

        def first(s, me):
            return (0, jnp.where(s - shift < 1, 1 - half, half), 0, 0, 0)

        def second(s, me):
            return (jnp.where(s - shift < 2, half, 1 - half), 0, 0, 0, 0)

        def third(s, me):
            low, high = self.place(s)
            return (high, low, 0, 0, 0)

        return [
            pl.BlockSpec((2, 1, deep, self.rows[0], self.cols), first),
            pl.BlockSpec((1, 2, deep, self.rows[1], self.cols), second),
            pl.BlockSpec((1, 1, deep, self.rows[2], self.cols), third),
        ]

    def out_shapes(self):
        return [
            jax.ShapeDtypeStruct((2, 2, self.zblocks // 2, r, self.cols), jnp.float32) for r in self.rows
        ]

    def multiply(self, s, lefts, high, low, outs, addends):
        s = s - self.shift

        def one(c):
            left = lefts[c][...]
            acc = jnp.dot(left, high(), preferred_element_type=jnp.float32)
            acc += jnp.dot(left, low(), preferred_element_type=jnp.float32)
            acc = acc.reshape(outs[c].shape)
            outs[c][...] = acc + addends[c][...] if addends else acc

        pl.when(jnp.logical_and(s >= 0, s < 2))(functools.partial(one, 0))
        pl.when(jnp.logical_and(s >= 1, s < 3))(functools.partial(one, 1))
        pl.when(s >= 0)(functools.partial(one, 2))

    def flops(self):
        return 4 * self.tokens * self.cols * self.zblocks * 2 * sum(self.rows)


def walk_kernel(walk, add, me_ref, a_ref, b_ref, c_ref, high_ref, low_ref, *rest):
    walk.multiply(
        pl.program_id(0),
        (a_ref, b_ref, c_ref),
        lambda: high_ref[...],
        lambda: low_ref[...],
        rest[-3:],
        rest[:3] if add else (),
    )


def products(half, core, lefts, high, low, me, expert_blocks, zblocks, addends=()):
    tokens, experts = high.shape
    cols = experts // expert_blocks
    walk = Walk(half, core, lefts, experts, cols, zblocks, 0)
    column = pl.BlockSpec((tokens, cols), lambda s, me: (0, walk.block_of(s, me[0])))
    outs = walk.out_specs()
    return pl.pallas_call(
        functools.partial(walk_kernel, walk, bool(addends)),
        grid_spec=pltpu.PrefetchScalarGridSpec(
            num_scalar_prefetch=1,
            grid=(4,),
            in_specs=walk.left_specs() + [column, column] + (outs if addends else []),
            out_specs=outs,
        ),
        out_shape=walk.out_shapes(),
        cost_estimate=pl.CostEstimate(
            flops=walk.flops(), bytes_accessed=4 * tokens * cols * 4 * 3, transcendentals=0
        ),
        name="products",
    )(me, *lefts, high, low, *addends)


def lead_kernel(walk, unit, blocks, me_ref, *refs):
    sources, lefts, (high_ref, low_ref), outs, (high_all, low_all, probs_ref) = (
        refs[:7], refs[7:10], refs[10:12], refs[12:15], refs[15:]
    )
    s = pl.program_id(0)

    @pl.when(s < blocks)
    def _():
        place = pl.ds(pl.multiple_of(s * LANES, LANES), LANES)

        def store(lanes, high, low):
            high_ref[:, lanes] = high
            low_ref[:, lanes] = low
            high_all[place, lanes] = high
            low_all[place, lanes] = low

        grad_block(unit, s, sources, probs_ref, store)

    low_bit, high_bit = walk.place(s)
    column = jnp.bitwise_xor(me_ref[0], walk.core + 2 * low_bit + 4 * high_bit)
    span = pl.ds(pl.multiple_of(column * walk.cols, LANES), walk.cols)
    walk.multiply(
        s,
        lefts,
        lambda: high_all[:, span],
        lambda: low_all[:, span],
        outs,
        (),
    )


def lead(logits, routed, stats, counts, keep_mask, unit, lefts, me, expert_blocks, zblocks):
    rows, experts = logits.shape
    blocks = rows // LANES
    cols = experts // expert_blocks
    walk = Walk(1, 1, lefts, experts, cols, zblocks, blocks)

    def row_block(s, me):
        return (jnp.minimum(s, blocks - 1), 0)

    wide = pl.BlockSpec((LANES, experts), row_block)
    thin = pl.BlockSpec((blocks, LANES), lambda s, me: (0, 0))
    flat = pl.BlockSpec((1, experts), lambda s, me: (0, 0))
    return pl.pallas_call(
        functools.partial(lead_kernel, walk, unit, blocks),
        grid_spec=pltpu.PrefetchScalarGridSpec(
            num_scalar_prefetch=1,
            grid=(blocks + 4,),
            in_specs=[wide, thin, thin, thin, thin, flat, flat] + walk.left_specs(),
            out_specs=[wide, wide] + walk.out_specs(),
            scratch_shapes=[pltpu.VMEM((rows, experts), jnp.bfloat16)] * 2
            + [pltpu.VMEM((LANES, experts), jnp.float32)],
        ),
        out_shape=[jax.ShapeDtypeStruct((rows, experts), jnp.bfloat16)] * 2 + walk.out_shapes(),
        cost_estimate=pl.CostEstimate(
            flops=walk.flops() + 2000 * rows * experts, bytes_accessed=12 * rows * experts, transcendentals=0
        ),
        name="lead",
    )(me, logits, routed, *stats, counts, keep_mask, *lefts)


def split_rows(rows, parts):
    tiles = rows // SUBLANES
    sizes = [tiles // parts + (1 if p < tiles % parts else 0) for p in range(parts)]
    return [s * SUBLANES for s in sizes]


def fits(tokens, router_logits):
    dp_width, expert_width = widths()
    rows, width = tokens.shape
    experts = router_logits.shape[1]
    bits = [w.bit_length() - 1 for w in (dp_width, expert_width)]
    powers = all(w == 1 << b for w, b in zip((dp_width, expert_width), bits))
    return (
        powers
        and bits[1] == 1 + 2
        and bits[0] == 2
        and width % (dp_width * SUBLANES) == 0
        and width // dp_width >= 3 * SUBLANES
        and experts % (expert_width * LANES) == 0
        and rows % LANES == 0
    )


def fallback(tokens, router_logits, gate_grad, expert_index, keep_mask, counts_here, unit):
    experts = router_logits.shape[1]
    counts = lax.psum(counts_here, ("dp", "expert")).reshape(1, experts)
    stats = softmax(router_logits, expert_index, gate_grad)
    high, low = logit_grad(router_logits, expert_index, stats, counts, keep_mask, unit)
    dims = (((0,), (0,)), ((), ()))
    partial = lax.dot_general(high, tokens, dims, preferred_element_type=jnp.float32)
    partial += lax.dot_general(low, tokens, dims, preferred_element_type=jnp.float32)
    owned = lax.psum_scatter(partial, "expert", scatter_dimension=0, tiled=True)
    return lax.psum_scatter(owned, "dp", scatter_dimension=1, tiled=True)


def local(tokens, router_logits, gate_grad, expert_index, keep_mask):
    dp_width, expert_width = widths()
    rows, width = tokens.shape
    experts = router_logits.shape[1]
    unit = experts / (rows * dp_width * expert_width)
    counts_here = local_counts(expert_index[:, 0], experts)
    expert_index = expert_index.reshape(rows // LANES, LANES)
    gate_grad = gate_grad.reshape(rows // LANES, LANES)
    keep_mask = keep_mask.reshape(1, experts)
    if not fits(tokens, router_logits):
        return fallback(tokens, router_logits, gate_grad, expert_index, keep_mask, counts_here, unit)

    counts = global_counts(counts_here).reshape(1, experts)
    stats = softmax(router_logits, expert_index, gate_grad)
    me = lax.axis_index("expert").astype(jnp.int32).reshape(1)
    me_dp = lax.axis_index("dp")
    zrows = width // dp_width
    low_bit, high_bit, near, far = ("expert", 1), ("expert", 2), ("dp", 0), ("dp", 1)
    orders = [
        (low_bit, near, high_bit, far),
        (high_bit, low_bit, near, far),
        (near, high_bit, low_bit, far),
    ]
    sizes = split_rows(zrows, len(orders))
    places = [near_bit + 2 * far_bit for near_bit in range(2) for far_bit in range(2)]
    pieces = [lax.dynamic_slice_in_dim(tokens, (me_dp ^ p) * zrows, zrows, 1).T for p in places]
    lefts = []
    offset = 0
    for size in sizes:
        lefts.append(jnp.concatenate([p[offset : offset + size] for p in pieces], axis=0))
        offset += size

    shared = dict(me=me, expert_blocks=expert_width, zblocks=dp_width)
    high, low, *away = lead(router_logits, expert_index, stats, counts, keep_mask, unit, lefts, **shared)
    arrived = [exchange(a, "expert", 1) for a in away]
    own = products(1, 0, lefts, high, low, **shared)
    sends = [o + r for o, r in zip(own, arrived)]
    sends, high, low = lax.optimization_barrier((sends, high, low))
    away = products(0, 1, lefts, high, low, **shared)
    rest = products(0, 0, lefts, high, low, addends=[exchange(a, "expert", 1) for a in away], **shared)
    held = [[r] for r in rest]
    for stage in range(len(orders[0])):
        for c, order in enumerate(orders):
            axis, bit = order[stage]
            held[c].append(exchange(sends[c], axis, 1 << bit))
        if stage == len(orders[0]) - 1:
            break
        for c in range(len(orders)):
            sends[c] = sum(h[1] for h in held[c][1:]) + held[c][0][1]
            held[c] = [h[0] for h in held[c]]
    out = jnp.concatenate([sum(h[1:], h[0]) for h in held], axis=0)
    return out.T


def solution(mesh):
    in_specs = (
        P(("dp", "expert"), None),
        P(("dp", "expert"), None),
        P(("dp", "expert")),
        P(("dp", "expert"), None),
        P(),
    )
    out_specs = P("expert", "dp")
    return jax.shard_map(local, mesh=mesh, in_specs=in_specs, out_specs=out_specs, check_vma=False)
```

time: 291 us -> 160 us (0.55)
  waiting for transfers between devices: 164 us -> 55.3 us
  Pallas kernels: 0 us -> 55.4 us
  blocking collectives: 42.1 us -> 0 us
  matrix products: 41.4 us -> 0.57 us
  starting transfers between devices: 0.04 us -> 27.6 us
  between operations: 13.4 us -> 0.18 us
  other arithmetic: 21.1 us -> 16.6 us
  local copies, waits for them, and re-layouts: 7.88 us -> 3.47 us
    reduce_scatter x2 -> x0, waiting for transfers between devices: 164 us -> none  [the longest x1 117 us: local(): lax.psum_scatter(make_term(logit_grad, wide_tokens), 'expert', scatter_di...]
    pallas_call x0 -> x5, Pallas kernels: none -> 55.4 us  [the longest x3 29.4 us: products(): pl.pallas_call(functools.partial(walk_kernel, walk, bool(addends)), grid_...]
    ppermute x0 -> x25, waiting for transfers between devices: none -> 55.3 us  [exchange(): return lax.ppermute(value, axis, [(i, i ^ mask) for i in range(size)])]
    psum x1 -> x0, blocking collectives: 42.1 us -> none  [local(): counts = lax.psum(local_counts, ('dp', 'expert'))]
    dot_general x3 -> x1, matrix products: 41.4 us -> 0.57 us  [local_counts(): lax.dot_general(high_hot, low_hot, (((0,), (0,)), ((), ())), preferred_el...]
    ppermute x0 -> x25, starting transfers between devices: none -> 27.6 us  [exchange(): return lax.ppermute(value, axis, [(i, i ^ mask) for i in range(size)])]
    add x0 -> x18, other arithmetic: none -> 11.4 us  [the longest x3 5.84 us: local(): sends = [o + r for o, r in zip(own, arrived)]]
    reduce_sum x7 -> x0, other arithmetic: 9.69 us -> none  [the longest x2 5.13 us: block_grad(): router_probs = weights / jnp.sum(weights, axis=1, keepdims=True)]
  transfers between devices with their start and end apart: 2 -> 25, of which waited for: 2 -> 13; matrix products, arithmetic and copies ran while one was open for 0% -> 10% of each run, Pallas kernels for 0% -> 17%
where the time goes in v1:
time: 160 us; the launch traced here: 159 us
  Pallas kernels  55.4 us (35%)
  waiting for transfers between devices  55.3 us (35%)
  starting transfers between devices  27.6 us (17%)
  other arithmetic  16.6 us (10%)
  local copies, waits for them, and re-layouts  3.47 us (2%)
    ppermute x25, waiting for transfers between devices, exchange(): return lax.ppermute(value, axis, [(i, i ^ mask) for i in range(size)])  55.3 us
    pallas_call x3, Pallas kernels, products(): pl.pallas_call(functools.partial(walk_kernel, walk, bool(addends)), grid_...  29.4 us
    ppermute x25, starting transfers between devices, exchange(): return lax.ppermute(value, axis, [(i, i ^ mask) for i in range(size)])  27.6 us
    pallas_call x1, Pallas kernels, lead(): pl.pallas_call(functools.partial(lead_kernel, walk, unit, blocks), grid_s...  18.8 us
    pallas_call x1, Pallas kernels, softmax(): pl.pallas_call(softmax_kernel, grid=(blocks,), in_specs=[wide, thin, thin...  7.28 us
    add x3, other arithmetic, local(): sends = [o + r for o, r in zip(own, arrived)]  5.84 us
    add x9, other arithmetic, local(): sends[c] = sum((h[1] for h in held[c][1:])) + held[c][0][1]  3.83 us
    concatenate x3, other arithmetic, local(): jnp.concatenate([p[offset:offset + size] for p in pieces], axis=0)  3.67 us
  transfers between devices with their start and end apart: 25, of which 13 were waited for; matrix products, arithmetic and copies ran while one was open for 10% of the time, Pallas kernels for 17%

profile of v1, /device:TPU:0, one launch (start us, length us, event | category | flops | bytes accessed | tf_op | source)
XLA Modules:
  0.0 159.2 jit_solution(16834571342873297634)
XLA Ops:
  0.0 0.7 and_select_fusion.1
  0.7 0.6 convolution_convert_fusion
  1.3 0.5 collective-permute-start
  1.8 2.7 %dynamic-slice_bitcast_fusion.3 = (bf16[520,1024]{1,0:T(8,128)(2,1)S(1)}, bf16[520,1024]{1,0:T(8,128)(2,1)S(1)}, bf16[520,1024]{1,0:T(8,128)(2,1)S(1)}, bf16[520,1024]{1,0:T(8,128)(2,1)S(1)}) fusion(bf16[1024,2080]{0,1:T(8,128)(2,1)} %param.5, s32[]{:T(128)S(6)} %select_n.26, s32[]{:T(128)S(6)} %select_n.27, s32[]{:T(128)S(6)} %select_n.29, s32[]{:T(128)S(6)} %select_n.28), kind=kLoop, calls=%fused_computation.7 | loop fusion | bytes 8519696 | tf_op jit(solution)/shard_map/transpose | solution.py:380
  4.7 1.2 pad_maximum_fusion.1.refs_8_.b_ref
  5.9 3.5 %collective-permute-start.3 = (s32[16,128]{1,0:T(8,128)S(1)}, s32[16,128]{1,0:T(8,128)S(1)}, u32[]{:S(2)}, u32[]{:S(2)}) collective-permute-start(s32[16,128]{1,0:T(8,128)S(1)} %add.164), channel_id=1, source_target_pairs={{0,6},{1,7},{2,4},{3,5},{4,2},{5,3},{6,0},{7,1},{8,14},{9,15},{10,... | collective-permute-start | bytes 24584 | tf_op jit(solution)/shard_map/ppermute | solution.py:33
  9.4 0.5 collective-permute-start.2
  10.1 1.3 pad_maximum_fusion.refs_7_.a_ref
  11.5 1.6 %collective-permute-done.2 = s32[16,128]{1,0:T(8,128)S(1)} collective-permute-done((s32[16,128]{1,0:T(8,128)S(1)}, s32[16,128]{1,0:T(8,128)S(1)}, u32[]{:S(2)}, u32[]{:S(2)}) %collective-permute-start.2) | collective-permute-done | bytes 8224 | tf_op jit(solution)/shard_map/ppermute | solution.py:33
  13.1 0.5 collective-permute-done.1
  13.6 3.6 %collective-permute-start.6 = (s32[16,128]{1,0:T(8,128)S(1)}, s32[16,128]{1,0:T(8,128)S(1)}, u32[]{:S(2)}, u32[]{:S(2)}) collective-permute-start(s32[16,128]{1,0:T(8,128)S(1)} %add_add_fusion.1), channel_id=1, source_target_pairs={{0,24},{8,16},{16,8},{24,0},{1,25},{9,17},{17,9},{25,1},{2,26},{10... | collective-permute-start | bytes 24584 | tf_op jit(solution)/shard_map/ppermute | solution.py:33
  17.2 0.8 collective-permute-start.4
  18.0 1.2 pad_maximum_fusion.2.refs_9_.c_ref
  19.2 7.3 %softmax.1 = (f32[8,128]{1,0:T(8,128)}, f32[8,128]{1,0:T(8,128)}, f32[8,128]{1,0:T(8,128)}) custom-call(bf16[1024,2048]{1,0:T(8,128)(2,1)} %refs_0_.1, s32[8,128]{1,0:T(8,128)} %bitcast.161, f32[8,128]{1,0:T(8,128)} %bitcast.166), custom_call_target="tpu_custom_call" | custom-call | flops 41943040 | bytes 4194304 | tf_op jit(solution)/shard_map/softmax/pallas_call | solution.py:89
  26.5 0.6 add_add_fusion
  27.1 18.8 %lead.1 = (bf16[1024,2048]{1,0:T(8,128)(2,1)}, bf16[1024,2048]{1,0:T(8,128)(2,1)}, f32[2,2,2,176,256]{4,3,2,1,0:T(8,128)}, f32[2,2,2,176,256]{4,3,2,1,0:T(8,128)}, f32[2,2,2,168,256]{4,3,2,1,0:T(8,128)}) custom-call(s32[1]{0:T(128)} %bitcast.me_ref, bf16[1024,2048]{1,0:T(8,128)(2,1)} %refs_0_.1, s32[8,128]{1,0:T(8,128)} %bitcast.162, ...), custom_call_target="tpu_custom_call" | custom-call | flops 8556380160 | bytes 25165824 | tf_op jit(solution)/shard_map/lead/pallas_call | solution.py:302
  45.9 0.5 collective-permute-start.8
  46.5 9.6 %products.3 = (f32[2,2,2,176,256]{4,3,2,1,0:T(8,128)}, f32[2,2,2,176,256]{4,3,2,1,0:T(8,128)}, f32[2,2,2,168,256]{4,3,2,1,0:T(8,128)}) custom-call(s32[1]{0:T(128)} %bitcast.me_ref, bf16[704,1024]{1,0:T(8,128)(2,1)} %pad_maximum_fusion.refs_7_.a_ref, bf16[704,1024]{1,0:T(8,128)(2,1)} %pad_maximum_fusion.1.refs_8_.b_ref, ...), custom_call_target="tpu_custom_call" | custom-call | flops 4362076160 | bytes 12582912 | tf_op jit(solution)/shard_map/products/pallas_call | solution.py:243
  56.1 3.2 %add.173 = f32[2,2,2,168,256]{4,3,2,1,0:T(8,128)} add(f32[2,2,2,168,256]{4,3,2,1,0:T(8,128)} %get-tuple-element.36, f32[2,2,2,168,256]{4,3,2,1,0:T(8,128)} %collective-permute-done.9) | non-fusion elementwise | flops 344064 | bytes 4128768 | tf_op jit(solution)/shard_map/add | solution.py:391
  59.2 1.4 add.171
  61.1 1.3 add.172
  62.4 9.5 %products.4 = (f32[2,2,2,176,256]{4,3,2,1,0:T(8,128)}, f32[2,2,2,176,256]{4,3,2,1,0:T(8,128)}, f32[2,2,2,168,256]{4,3,2,1,0:T(8,128)}) custom-call(s32[1]{0:T(128)} %bitcast.me_ref, bf16[704,1024]{1,0:T(8,128)(2,1)} %pad_maximum_fusion.refs_7_.a_ref, bf16[704,1024]{1,0:T(8,128)(2,1)} %pad_maximum_fusion.1.refs_8_.b_ref, ...), custom_call_target="tpu_custom_call" | custom-call | flops 4362076160 | bytes 12582912 | tf_op jit(solution)/shard_map/products/pallas_call | solution.py:243
  72.9 1.2 collective-permute-start.21
  74.1 1.5 collective-permute-start.17
  75.6 0.6 collective-permute-start.13
  76.2 1.3 collective-permute-done.10.rest_0_
  77.5 2.1 %collective-permute-done.11.rest_1_ = f32[2,2,2,176,256]{4,3,2,1,0:T(8,128)} collective-permute-done((f32[2,2,2,176,256]{4,3,2,1,0:T(8,128)}, f32[2,2,2,176,256]{4,3,2,1,0:T(8,128)}, u32[]{:S(2)}, u32[]{:S(2)}) %collective-permute-start.11) | collective-permute-done | bytes 1441824 | tf_op jit(solution)/shard_map/ppermute | solution.py:33
  79.6 10.2 %products.5 = (f32[2,2,2,176,256]{4,3,2,1,0:T(8,128)}, f32[2,2,2,176,256]{4,3,2,1,0:T(8,128)}, f32[2,2,2,168,256]{4,3,2,1,0:T(8,128)}) custom-call(s32[1]{0:T(128)} %bitcast.me_ref, bf16[704,1024]{1,0:T(8,128)(2,1)} %pad_maximum_fusion.refs_7_.a_ref, bf16[704,1024]{1,0:T(8,128)(2,1)} %pad_maximum_fusion.1.refs_8_.b_ref, ...), custom_call_target="tpu_custom_call" | custom-call | flops 4362076160 | bytes 12582912 | tf_op jit(solution)/shard_map/products/pallas_call | solution.py:243
  89.8 15.5 %collective-permute-done.21 = f32[2,2,2,168,256]{4,3,2,1,0:T(8,128)} collective-permute-done((f32[2,2,2,168,256]{4,3,2,1,0:T(8,128)}, f32[2,2,2,168,256]{4,3,2,1,0:T(8,128)}, u32[]{:S(2)}, u32[]{:S(2)}) %collective-permute-start.21) | collective-permute-done | bytes 1376288 | tf_op jit(solution)/shard_map/ppermute | solution.py:33
  105.4 1.4 fusion.2
  106.8 1.6 %collective-permute-start.22 = (f32[2,2,168,256]{3,2,1,0:T(8,128)S(1)}, f32[2,2,168,256]{3,2,1,0:T(8,128)S(1)}, u32[]{:S(2)}, u32[]{:S(2)}) collective-permute-start(f32[2,2,168,256]{3,2,1,0:T(8,128)S(1)} %fusion.2), channel_id=1, source_target_pairs={{0,4},{1,5},{2,6},{3,7},{4,0},{5,1},{6,2},{7,3},{8,12},{9,13},{10,... | collective-permute-start | bytes 2064392 | tf_op jit(solution)/shard_map/ppermute | solution.py:33
  108.5 0.6 collective-permute-start.18
  109.6 1.3 collective-permute-start.14
  110.9 12.4 %collective-permute-done.22 = f32[2,2,168,256]{3,2,1,0:T(8,128)S(1)} collective-permute-done((f32[2,2,168,256]{3,2,1,0:T(8,128)S(1)}, f32[2,2,168,256]{3,2,1,0:T(8,128)S(1)}, u32[]{:S(2)}, u32[]{:S(2)}) %collective-permute-start.22) | collective-permute-done | bytes 688160 | tf_op jit(solution)/shard_map/ppermute | solution.py:33
  123.4 1.0 fusion.8
  124.9 0.9 collective-permute-done.18
  125.9 1.3 collective-permute-start.19
  127.7 2.5 %collective-permute-start.15 = (f32[2,176,256]{2,1,0:T(8,128)S(1)}, f32[2,176,256]{2,1,0:T(8,128)S(1)}, u32[]{:S(2)}, u32[]{:S(2)}) collective-permute-start(f32[2,176,256]{2,1,0:T(8,128)S(1)} %fusion.6), channel_id=1, source_target_pairs={{0,4},{1,5},{2,6},{3,7},{4,0},{5,1},{6,2},{7,3},{8,12},{9,13},{10,... | collective-permute-start | bytes 1081352 | tf_op jit(solution)/shard_map/ppermute | solution.py:33
  130.2 2.8 %collective-permute-done.23 = f32[2,168,256]{2,1,0:T(8,128)S(1)} collective-permute-done((f32[2,168,256]{2,1,0:T(8,128)S(1)}, f32[2,168,256]{2,1,0:T(8,128)S(1)}, u32[]{:S(2)}, u32[]{:S(2)}) %collective-permute-start.23) | collective-permute-done | bytes 344096 | tf_op jit(solution)/shard_map/ppermute | solution.py:33
  133.0 1.0 fusion.26
  134.0 2.9 %collective-permute-start.24 = (f32[168,256]{1,0:T(8,128)S(1)}, f32[168,256]{1,0:T(8,128)S(1)}, u32[]{:S(2)}, u32[]{:S(2)}) collective-permute-start(f32[168,256]{1,0:T(8,128)S(1)} %fusion.26), channel_id=1, source_target_pairs={{0,16},{8,24},{16,0},{24,8},{1,17},{9,25},{17,1},{25,9},{2,18},{10... | collective-permute-start | bytes 516104 | tf_op jit(solution)/shard_map/ppermute | solution.py:33
  136.9 1.3 collective-permute-start.20
  138.2 1.8 %collective-permute-start.16 = (f32[176,256]{1,0:T(8,128)S(1)}, f32[176,256]{1,0:T(8,128)S(1)}, u32[]{:S(2)}, u32[]{:S(2)}) collective-permute-start(f32[176,256]{1,0:T(8,128)S(1)} %fusion.19), channel_id=1, source_target_pairs={{0,16},{8,24},{16,0},{24,8},{1,17},{9,25},{17,1},{25,9},{2,18},{10... | collective-permute-start | bytes 540680 | tf_op jit(solution)/shard_map/ppermute | solution.py:33
  140.0 12.0 %collective-permute-done.24 = f32[168,256]{1,0:T(8,128)S(1)} collective-permute-done((f32[168,256]{1,0:T(8,128)S(1)}, f32[168,256]{1,0:T(8,128)S(1)}, u32[]{:S(2)}, u32[]{:S(2)}) %collective-permute-start.24) | collective-permute-done | bytes 172064 | tf_op jit(solution)/shard_map/ppermute | solution.py:33
  152.0 1.0 fusion.29
  153.0 2.9 %collective-permute-done.20 = f32[176,256]{1,0:T(8,128)S(1)} collective-permute-done((f32[176,256]{1,0:T(8,128)S(1)}, f32[176,256]{1,0:T(8,128)S(1)}, u32[]{:S(2)}, u32[]{:S(2)}) %collective-permute-start.20) | collective-permute-done | bytes 180256 | tf_op jit(solution)/shard_map/ppermute | solution.py:33
  156.0 2.3 %collective-permute-done.16 = f32[176,256]{1,0:T(8,128)S(1)} collective-permute-done((f32[176,256]{1,0:T(8,128)S(1)}, f32[176,256]{1,0:T(8,128)S(1)}, u32[]{:S(2)}, u32[]{:S(2)}) %collective-permute-start.16) | collective-permute-done | bytes 180256 | tf_op jit(solution)/shard_map/ppermute | solution.py:33
  158.4 0.8 maximum_bitcast_fusion
  (49 shorter events, 4.0 us)
Async XLA Ops:
  1.3 4.6 %collective-permute-start = (s32[16,128]{1,0:T(8,128)S(1)}, s32[16,128]{1,0:T(8,128)S(1)}, u32[]{:S(2)}, u32[]{:S(2)}) collective-permute-start(s32[16,128]{1,0:T(8,128)S(1)} %convolution_convert_fusion), channel_id=1, source_target_pairs={{0,1},{1,0},{2,3},{3,2},{4,5},{5,4},{6,7},{7,6},{8,9},{9,8},{10,11... | collective-permute-start | bytes 24584 | tf_op jit(solution)/shard_map/ppermute | solution.py:33
  5.9 5.5 %collective-permute-start.3 = (s32[16,128]{1,0:T(8,128)S(1)}, s32[16,128]{1,0:T(8,128)S(1)}, u32[]{:S(2)}, u32[]{:S(2)}) collective-permute-start(s32[16,128]{1,0:T(8,128)S(1)} %add.164), channel_id=1, source_target_pairs={{0,6},{1,7},{2,4},{3,5},{4,2},{5,3},{6,0},{7,1},{8,14},{9,15},{10,... | collective-permute-start | bytes 24584 | tf_op jit(solution)/shard_map/ppermute | solution.py:33
  9.4 3.7 %collective-permute-start.2 = (s32[16,128]{1,0:T(8,128)S(1)}, s32[16,128]{1,0:T(8,128)S(1)}, u32[]{:S(2)}, u32[]{:S(2)}) collective-permute-start(s32[16,128]{1,0:T(8,128)S(1)} %add.164), channel_id=1, source_target_pairs={{0,4},{1,5},{2,6},{3,7},{4,0},{5,1},{6,2},{7,3},{8,12},{9,13},{10,... | collective-permute-start | bytes 24584 | tf_op jit(solution)/shard_map/ppermute | solution.py:33
  9.9 3.7 %collective-permute-start.1 = (s32[16,128]{1,0:T(8,128)S(1)}, s32[16,128]{1,0:T(8,128)S(1)}, u32[]{:S(2)}, u32[]{:S(2)}) collective-permute-start(s32[16,128]{1,0:T(8,128)S(1)} %add.164), channel_id=1, source_target_pairs={{0,2},{1,3},{2,0},{3,1},{4,6},{5,7},{6,4},{7,5},{8,10},{9,11},{10,... | collective-permute-start | bytes 24584 | tf_op jit(solution)/shard_map/ppermute | solution.py:33
  13.6 12.9 %collective-permute-start.6 = (s32[16,128]{1,0:T(8,128)S(1)}, s32[16,128]{1,0:T(8,128)S(1)}, u32[]{:S(2)}, u32[]{:S(2)}) collective-permute-start(s32[16,128]{1,0:T(8,128)S(1)} %add_add_fusion.1), channel_id=1, source_target_pairs={{0,24},{8,16},{16,8},{24,0},{1,25},{9,17},{17,9},{25,1},{2,26},{10... | collective-permute-start | bytes 24584 | tf_op jit(solution)/shard_map/ppermute | solution.py:33
  17.2 9.3 %collective-permute-start.5 = (s32[16,128]{1,0:T(8,128)S(1)}, s32[16,128]{1,0:T(8,128)S(1)}, u32[]{:S(2)}, u32[]{:S(2)}) collective-permute-start(s32[16,128]{1,0:T(8,128)S(1)} %add_add_fusion.1), channel_id=1, source_target_pairs={{0,16},{8,24},{16,0},{24,8},{1,17},{9,25},{17,1},{25,9},{2,18},{10... | collective-permute-start | bytes 24584 | tf_op jit(solution)/shard_map/ppermute | solution.py:33
  17.2 9.3 %collective-permute-start.4 = (s32[16,128]{1,0:T(8,128)S(1)}, s32[16,128]{1,0:T(8,128)S(1)}, u32[]{:S(2)}, u32[]{:S(2)}) collective-permute-start(s32[16,128]{1,0:T(8,128)S(1)} %add_add_fusion.1), channel_id=1, source_target_pairs={{0,8},{8,0},{16,24},{24,16},{1,9},{9,1},{17,25},{25,17},{2,10},{10... | collective-permute-start | bytes 24584 | tf_op jit(solution)/shard_map/ppermute | solution.py:33
  45.9 13.3 %collective-permute-start.7 = (f32[2,2,2,176,256]{4,3,2,1,0:T(8,128)}, f32[2,2,2,176,256]{4,3,2,1,0:T(8,128)S(1)}, u32[]{:S(2)}, u32[]{:S(2)}) collective-permute-start(f32[2,2,2,176,256]{4,3,2,1,0:T(8,128)} %get-tuple-element.33), channel_id=1, source_target_pairs={{0,1},{1,0},{2,3},{3,2},{4,5},{5,4},{6,7},{7,6},{8,9},{9,8},{10,11... | collective-permute-start | bytes 4325384 | tf_op jit(solution)/shard_map/ppermute | solution.py:33
  45.9 14.7 %collective-permute-start.8 = (f32[2,2,2,176,256]{4,3,2,1,0:T(8,128)}, f32[2,2,2,176,256]{4,3,2,1,0:T(8,128)S(1)}, u32[]{:S(2)}, u32[]{:S(2)}) collective-permute-start(f32[2,2,2,176,256]{4,3,2,1,0:T(8,128)} %get-tuple-element.35), channel_id=1, source_target_pairs={{0,1},{1,0},{2,3},{3,2},{4,5},{5,4},{6,7},{7,6},{8,9},{9,8},{10,11... | collective-permute-start | bytes 4325384 | tf_op jit(solution)/shard_map/ppermute | solution.py:33
  46.4 9.7 %collective-permute-start.9 = (f32[2,2,2,168,256]{4,3,2,1,0:T(8,128)}, f32[2,2,2,168,256]{4,3,2,1,0:T(8,128)}, u32[]{:S(2)}, u32[]{:S(2)}) collective-permute-start(f32[2,2,2,168,256]{4,3,2,1,0:T(8,128)} %get-tuple-element.37), channel_id=1, source_target_pairs={{0,1},{1,0},{2,3},{3,2},{4,5},{5,4},{6,7},{7,6},{8,9},{9,8},{10,11... | collective-permute-start | bytes 4128776 | tf_op jit(solution)/shard_map/ppermute | solution.py:33
  56.1 3.2 %copy-start.3 = (f32[2,2,2,176,256]{4,3,2,1,0:T(8,128)S(1)}, f32[2,2,2,176,256]{4,3,2,1,0:T(8,128)}, u32[]{:S(2)}) copy-start(f32[2,2,2,176,256]{4,3,2,1,0:T(8,128)} %get-tuple-element.32) | copy-start | bytes 4325380
  59.2 1.9 %copy-start.2 = (f32[2,2,2,176,256]{4,3,2,1,0:T(8,128)S(1)}, f32[2,2,2,176,256]{4,3,2,1,0:T(8,128)}, u32[]{:S(2)}) copy-start(f32[2,2,2,176,256]{4,3,2,1,0:T(8,128)} %get-tuple-element.34) | copy-start | bytes 4325380
  71.9 3.7 %collective-permute-start.12 = (f32[2,2,2,168,256]{4,3,2,1,0:T(8,128)}, f32[2,2,2,168,256]{4,3,2,1,0:T(8,128)}, u32[]{:S(2)}, u32[]{:S(2)}) collective-permute-start(f32[2,2,2,168,256]{4,3,2,1,0:T(8,128)} %get-tuple-element.42), channel_id=1, source_target_pairs={{0,1},{1,0},{2,3},{3,2},{4,5},{5,4},{6,7},{7,6},{8,9},{9,8},{10,11... | collective-permute-start | bytes 4128776 | tf_op jit(solution)/shard_map/ppermute | solution.py:33
  72.4 5.2 %collective-permute-start.10 = (f32[2,2,2,176,256]{4,3,2,1,0:T(8,128)}, f32[2,2,2,176,256]{4,3,2,1,0:T(8,128)}, u32[]{:S(2)}, u32[]{:S(2)}) collective-permute-start(f32[2,2,2,176,256]{4,3,2,1,0:T(8,128)} %get-tuple-element.40), channel_id=1, source_target_pairs={{0,1},{1,0},{2,3},{3,2},{4,5},{5,4},{6,7},{7,6},{8,9},{9,8},{10,11... | collective-permute-start | bytes 4325384 | tf_op jit(solution)/shard_map/ppermute | solution.py:33
  72.4 7.1 %collective-permute-start.11 = (f32[2,2,2,176,256]{4,3,2,1,0:T(8,128)}, f32[2,2,2,176,256]{4,3,2,1,0:T(8,128)}, u32[]{:S(2)}, u32[]{:S(2)}) collective-permute-start(f32[2,2,2,176,256]{4,3,2,1,0:T(8,128)} %get-tuple-element.41), channel_id=1, source_target_pairs={{0,1},{1,0},{2,3},{3,2},{4,5},{5,4},{6,7},{7,6},{8,9},{9,8},{10,11... | collective-permute-start | bytes 4325384 | tf_op jit(solution)/shard_map/ppermute | solution.py:33
  72.9 32.5 %collective-permute-start.21 = (f32[2,2,2,168,256]{4,3,2,1,0:T(8,128)}, f32[2,2,2,168,256]{4,3,2,1,0:T(8,128)}, u32[]{:S(2)}, u32[]{:S(2)}) collective-permute-start(f32[2,2,2,168,256]{4,3,2,1,0:T(8,128)} %add.173), channel_id=1, source_target_pairs={{0,8},{8,0},{16,24},{24,16},{1,9},{9,1},{17,25},{25,17},{2,10},{10... | collective-permute-start | bytes 4128776 | tf_op jit(solution)/shard_map/ppermute | solution.py:33
  74.1 34.3 %collective-permute-start.17 = (f32[2,2,2,176,256]{4,3,2,1,0:T(8,128)}, f32[2,2,2,176,256]{4,3,2,1,0:T(8,128)S(1)}, u32[]{:S(2)}, u32[]{:S(2)}) collective-permute-start(f32[2,2,2,176,256]{4,3,2,1,0:T(8,128)} %add.172), channel_id=1, source_target_pairs={{0,4},{1,5},{2,6},{3,7},{4,0},{5,1},{6,2},{7,3},{8,12},{9,13},{10,... | collective-permute-start | bytes 4325384 | tf_op jit(solution)/shard_map/ppermute | solution.py:33
  75.6 33.9 %collective-permute-start.13 = (f32[2,2,2,176,256]{4,3,2,1,0:T(8,128)}, f32[2,2,2,176,256]{4,3,2,1,0:T(8,128)S(1)}, u32[]{:S(2)}, u32[]{:S(2)}) collective-permute-start(f32[2,2,2,176,256]{4,3,2,1,0:T(8,128)} %add.171), channel_id=1, source_target_pairs={{0,2},{1,3},{2,0},{3,1},{4,6},{5,7},{6,4},{7,5},{8,10},{9,11},{10,... | collective-permute-start | bytes 4325384 | tf_op jit(solution)/shard_map/ppermute | solution.py:33
  89.8 18.6 %copy-start.1 = (f32[2,2,2,176,256]{4,3,2,1,0:T(8,128)S(1)}, f32[2,2,2,176,256]{4,3,2,1,0:T(8,128)}, u32[]{:S(2)}) copy-start(f32[2,2,2,176,256]{4,3,2,1,0:T(8,128)} %get-tuple-element.45) | copy-start | bytes 4325380
  106.8 2.8 %copy-start = (f32[2,2,2,176,256]{4,3,2,1,0:T(8,128)S(1)}, f32[2,2,2,176,256]{4,3,2,1,0:T(8,128)}, u32[]{:S(2)}) copy-start(f32[2,2,2,176,256]{4,3,2,1,0:T(8,128)} %get-tuple-element.43) | copy-start | bytes 4325380
  106.8 16.6 %collective-permute-start.22 = (f32[2,2,168,256]{3,2,1,0:T(8,128)S(1)}, f32[2,2,168,256]{3,2,1,0:T(8,128)S(1)}, u32[]{:S(2)}, u32[]{:S(2)}) collective-permute-start(f32[2,2,168,256]{3,2,1,0:T(8,128)S(1)} %fusion.2), channel_id=1, source_target_pairs={{0,4},{1,5},{2,6},{3,7},{4,0},{5,1},{6,2},{7,3},{8,12},{9,13},{10,... | collective-permute-start | bytes 2064392 | tf_op jit(solution)/shard_map/ppermute | solution.py:33
  108.5 14.9 %copy-start.4 = (f32[2,2,2,168,256]{4,3,2,1,0:T(8,128)S(1)}, f32[2,2,2,168,256]{4,3,2,1,0:T(8,128)}, u32[]{:S(2)}) copy-start(f32[2,2,2,168,256]{4,3,2,1,0:T(8,128)} %get-tuple-element.47) | copy-start | bytes 4128772
  108.5 17.3 %collective-permute-start.18 = (f32[2,2,176,256]{3,2,1,0:T(8,128)S(1)}, f32[2,2,176,256]{3,2,1,0:T(8,128)S(1)}, u32[]{:S(2)}, u32[]{:S(2)}) collective-permute-start(f32[2,2,176,256]{3,2,1,0:T(8,128)S(1)} %fusion), channel_id=1, source_target_pairs={{0,2},{1,3},{2,0},{3,1},{4,6},{5,7},{6,4},{7,5},{8,10},{9,11},{10,... | collective-permute-start | bytes 2162696 | tf_op jit(solution)/shard_map/ppermute | solution.py:33
  109.6 18.0 %collective-permute-start.14 = (f32[2,2,176,256]{3,2,1,0:T(8,128)S(1)}, f32[2,2,176,256]{3,2,1,0:T(8,128)S(1)}, u32[]{:S(2)}, u32[]{:S(2)}) collective-permute-start(f32[2,2,176,256]{3,2,1,0:T(8,128)S(1)} %fusion.1), channel_id=1, source_target_pairs={{0,8},{8,0},{16,24},{24,16},{1,9},{9,1},{17,25},{25,17},{2,10},{10... | collective-permute-start | bytes 2162696 | tf_op jit(solution)/shard_map/ppermute | solution.py:33
  124.4 8.6 %collective-permute-start.23 = (f32[2,168,256]{2,1,0:T(8,128)S(1)}, f32[2,168,256]{2,1,0:T(8,128)S(1)}, u32[]{:S(2)}, u32[]{:S(2)}) collective-permute-start(f32[2,168,256]{2,1,0:T(8,128)S(1)} %fusion.8), channel_id=1, source_target_pairs={{0,2},{1,3},{2,0},{3,1},{4,6},{5,7},{6,4},{7,5},{8,10},{9,11},{10,... | collective-permute-start | bytes 1032200 | tf_op jit(solution)/shard_map/ppermute | solution.py:33
  125.9 11.0 %collective-permute-start.19 = (f32[2,176,256]{2,1,0:T(8,128)S(1)}, f32[2,176,256]{2,1,0:T(8,128)S(1)}, u32[]{:S(2)}, u32[]{:S(2)}) collective-permute-start(f32[2,176,256]{2,1,0:T(8,128)S(1)} %fusion.4), channel_id=1, source_target_pairs={{0,8},{8,0},{16,24},{24,16},{1,9},{9,1},{17,25},{25,17},{2,10},{10... | collective-permute-start | bytes 1081352 | tf_op jit(solution)/shard_map/ppermute | solution.py:33
  127.7 10.5 %collective-permute-start.15 = (f32[2,176,256]{2,1,0:T(8,128)S(1)}, f32[2,176,256]{2,1,0:T(8,128)S(1)}, u32[]{:S(2)}, u32[]{:S(2)}) collective-permute-start(f32[2,176,256]{2,1,0:T(8,128)S(1)} %fusion.6), channel_id=1, source_target_pairs={{0,4},{1,5},{2,6},{3,7},{4,0},{5,1},{6,2},{7,3},{8,12},{9,13},{10,... | collective-permute-start | bytes 1081352 | tf_op jit(solution)/shard_map/ppermute | solution.py:33
  134.0 18.1 %collective-permute-start.24 = (f32[168,256]{1,0:T(8,128)S(1)}, f32[168,256]{1,0:T(8,128)S(1)}, u32[]{:S(2)}, u32[]{:S(2)}) collective-permute-start(f32[168,256]{1,0:T(8,128)S(1)} %fusion.26), channel_id=1, source_target_pairs={{0,16},{8,24},{16,0},{24,8},{1,17},{9,25},{17,1},{25,9},{2,18},{10... | collective-permute-start | bytes 516104 | tf_op jit(solution)/shard_map/ppermute | solution.py:33
  136.9 19.0 %collective-permute-start.20 = (f32[176,256]{1,0:T(8,128)S(1)}, f32[176,256]{1,0:T(8,128)S(1)}, u32[]{:S(2)}, u32[]{:S(2)}) collective-permute-start(f32[176,256]{1,0:T(8,128)S(1)} %fusion.12), channel_id=1, source_target_pairs={{0,16},{8,24},{16,0},{24,8},{1,17},{9,25},{17,1},{25,9},{2,18},{10... | collective-permute-start | bytes 540680 | tf_op jit(solution)/shard_map/ppermute | solution.py:33
  138.2 20.1 %collective-permute-start.16 = (f32[176,256]{1,0:T(8,128)S(1)}, f32[176,256]{1,0:T(8,128)S(1)}, u32[]{:S(2)}, u32[]{:S(2)}) collective-permute-start(f32[176,256]{1,0:T(8,128)S(1)} %fusion.19), channel_id=1, source_target_pairs={{0,16},{8,24},{16,0},{24,8},{1,17},{9,25},{17,1},{25,9},{2,18},{10... | collective-permute-start | bytes 540680 | tf_op jit(solution)/shard_map/ppermute | solution.py:33
